TPU v7x, 32 devices: a whole 2x2x4 slice. The times are simulated.
32 devices in a mesh: gx: 4 (over x, core), gy: 8 (over z, y).
Axes of the slice: x: 2, y: 2, z: 4, core: 2. Of those that a mesh axis runs over, the one named last changes fastest.
Arguments:
- krylov_basis: float32 [144, 32, 64, 256], P(None, 'gx', 'gy'), may hold values from -6 to 6
- advection: float32 [3, 32, 64, 256], P(None, 'gx', 'gy'), may hold values from -0.6 to 0.6
- reaction: float32 [32, 64, 256], P('gx', 'gy'), may hold values from 0.1 to 2
Outputs:
- block_one: float32 [16, 32, 64, 256], P(None, 'gx', 'gy')
- block_two: float32 [16, 32, 64, 256], P(None, 'gx', 'gy')
- coeff_one: float32 [144, 16], replicated
- coeff_two: float32 [160, 16], replicated
- upper_one: float32 [16, 16], replicated
- upper_two: float32 [16, 16], replicated
All inputs are finite; a program needn't handle non-finite values.
Results may differ from a plain program's by a relative error of at most 0.0003.
Values sent between devices are 32-bit elements; how exact they have to be, the bound alone decides.
A program may use at most 128 MiB of HBM per device.

v0:
```python
import functools

import jax
import jax.numpy as jnp
from jax import lax
from jax.experimental import pallas as pl
from jax.experimental.pallas import tpu as pltpu
from jax.sharding import PartitionSpec as P

BLOCK = 16
LANES = 128
WIDE = 256
MESH = pl.DeviceIdType.MESH
HIGHEST = lax.Precision.HIGHEST
F32 = jnp.float32
BF16 = jnp.bfloat16


def exact(left, right, nt=False):
    dims = (((1,), (1 if nt else 0,)), ((), ()))
    return lax.dot_general(left, right, dims, precision=HIGHEST, preferred_element_type=F32)


def quick(left, right, nt=False):
    dims = (((1,), (1 if nt else 0,)), ((), ()))
    return lax.dot_general(left, right, dims, preferred_element_type=F32)


def split(values):
    high = values.astype(BF16)
    low = (values - high.astype(F32)).astype(BF16)
    return high, low


def sum_everywhere(nx, ny, own, first, part, second, done, whole, sems):
    gx, gy = lax.axis_index("gx"), lax.axis_index("gy")
    height = part.shape[0]
    send1, recv1, send2, recv2, send3, recv3 = sems
    mine = pl.ds(pl.multiple_of(gx * height, 8), height)
    copies = []
    for d in range(1, nx):
        peer = lax.rem(gx + d, nx)
        copies.append(
            pltpu.make_async_remote_copy(
                src_ref=own.at[pl.ds(pl.multiple_of(peer * height, 8), height)],
                dst_ref=first.at[d - 1],
                send_sem=send1.at[d - 1],
                recv_sem=recv1.at[d - 1],
                device_id=(peer, gy),
                device_id_type=MESH,
            )
        )
    for copy in copies:
        copy.start()
    for copy in copies:
        copy.wait_recv()
    total = own[mine, :]
    for d in range(1, nx):
        total = total + first[d - 1]
    part[...] = total
    second[gy] = total
    across = []
    for d in range(1, ny):
        peer = lax.rem(gy + d, ny)
        across.append(
            pltpu.make_async_remote_copy(
                src_ref=part,
                dst_ref=second.at[gy],
                send_sem=send2.at[d - 1],
                recv_sem=recv2.at[d - 1],
                device_id=(gx, peer),
                device_id_type=MESH,
            )
        )
    for copy in across:
        copy.start()
    for copy in across:
        copy.wait_recv()
    total = second[0]
    for s in range(1, ny):
        total = total + second[s]
    done[...] = total
    whole[mine, :] = total
    back = []
    for d in range(1, nx):
        peer = lax.rem(gx + d, nx)
        back.append(
            pltpu.make_async_remote_copy(
                src_ref=done,
                dst_ref=whole.at[mine],
                send_sem=send3.at[d - 1],
                recv_sem=recv3.at[d - 1],
                device_id=(peer, gy),
                device_id_type=MESH,
            )
        )
    for copy in back:
        copy.start()
    for copy in back:
        copy.wait_recv()
    for copy in copies + across + back:
        copy.wait_send()


def factor(gram):
    n = gram.shape[0]
    row = lax.broadcasted_iota(jnp.int32, (n, n), 0)
    col = lax.broadcasted_iota(jnp.int32, (n, n), 1)
    both = jnp.concatenate([gram, (row == col).astype(F32)], axis=1)
    wide_row = lax.broadcasted_iota(jnp.int32, (n, 2 * n), 0)
    for k in range(n):
        scale = 1.0 / jnp.sqrt(both[k : k + 1, k : k + 1])
        pivot = both[k : k + 1, :] * scale
        column = both[:, k : k + 1] * scale
        both = jnp.where(
            wide_row > k, both - column * pivot, jnp.where(wide_row == k, pivot, both)
        )
    return jnp.where(col >= row, both[:, :n], 0.0), both[:, n:]


def solve_small(count, sums, metric, cells):
    col = lax.broadcasted_iota(jnp.int32, (BLOCK, WIDE), 1)
    row = lax.broadcasted_iota(jnp.int32, (BLOCK, WIDE), 0)
    sums = sums * (1.0 / cells)
    first = jnp.where(col < count, sums, 0.0)
    square = sums[:, count : count + BLOCK]
    coeff = 2.0 * first - exact(first, metric)
    seen = exact(coeff, metric)
    gram = square - 2.0 * exact(coeff, first, nt=True) + exact(seen, coeff, nt=True)
    upper, inverse = factor(gram)
    pick = jnp.where(col == row + count, 1.0, 0.0)
    combine = exact(inverse, pick - coeff)
    left = exact(inverse, first - seen)
    return coeff, upper, combine, left


def kernel(
    nx, ny,
    v_hbm, adv, rea,
    one_hbm, two_hbm, coeff1, coeff2, upper1, upper2,
    vf, bh, bl, uf, qf, pf, acc, hacc, metric,
    own1, first1, part1, second1, done1, whole1,
    own2, first2, part2, second2, done2, whole2,
    vsem, usem, osem1, osem2, hs1, hr1, hs2, hr2,
    *sems,
):
    rows, X, Y, Z = v_hbm.shape
    main = rows - BLOCK
    cells = float(X * Y * Z * nx * ny)
    gx, gy = lax.axis_index("gx"), lax.axis_index("gy")

    def load_u(p):
        x, y = p // Y, p % Y
        return pltpu.make_async_copy(
            v_hbm.at[pl.ds(main, BLOCK), x, y], uf.at[x + 1, y + 1], usem.at[p]
        )

    def load_v(p):
        x, y = p // Y, p % Y
        return pltpu.make_async_copy(v_hbm.at[pl.ds(0, main), x, y], vf.at[p], vsem.at[p])

    def loop(n, f):
        lax.fori_loop(0, n, lambda i, c: (f(i), c)[1], 0)

    loop(X * Y, lambda p: load_u(p).start())
    loop(X * Y, lambda p: load_v(p).start())

    barrier = pltpu.get_barrier_semaphore()
    for d in range(1, nx):
        pl.semaphore_signal(
            barrier, inc=1, device_id=(lax.rem(gx + d, nx), gy), device_id_type=MESH
        )
    for d in range(1, ny):
        pl.semaphore_signal(
            barrier, inc=1, device_id=(gx, lax.rem(gy + d, ny)), device_id_type=MESH
        )

    acc[...] = jnp.zeros_like(acc)
    hacc[...] = jnp.zeros_like(hacc)
    metric[...] = jnp.zeros_like(metric)
    own1[...] = jnp.zeros_like(own1)
    own2[...] = jnp.zeros_like(own2)
    edge_x = jnp.zeros((1, Y, BLOCK, Z), F32)
    edge_y = jnp.zeros((X, 1, BLOCK, Z), F32)
    for field in (uf, qf):

        @pl.when(gx == 0)
        def _(field=field):
            field[0:1, 1 : Y + 1] = edge_x

        @pl.when(gx == nx - 1)
        def _(field=field):
            field[X + 1 : X + 2, 1 : Y + 1] = edge_x

        @pl.when(gy == 0)
        def _(field=field):
            field[1 : X + 1, 0:1] = edge_y

        @pl.when(gy == ny - 1)
        def _(field=field):
            field[1 : X + 1, Y + 1 : Y + 2] = edge_y

    def borders(field, ss, rs):
        xs, ys = pl.ds(1, X), pl.ds(1, Y)
        up, down = lax.rem(gx + 1, nx), lax.rem(gx + nx - 1, nx)
        right, left = lax.rem(gy + 1, ny), lax.rem(gy + ny - 1, ny)

        def make(i, src, dst, dev):
            return pltpu.make_async_remote_copy(
                src_ref=src, dst_ref=dst, send_sem=ss.at[i], recv_sem=rs.at[i],
                device_id=dev, device_id_type=MESH,
            )

        return (
            (gx < nx - 1, gx > 0, make(0, field.at[X, ys], field.at[0, ys], (up, gy))),
            (gx > 0, gx < nx - 1, make(1, field.at[1, ys], field.at[X + 1, ys], (down, gy))),
            (gy < ny - 1, gy > 0, make(2, field.at[xs, Y], field.at[xs, 0], (gx, right))),
            (gy > 0, gy < ny - 1, make(3, field.at[xs, 1], field.at[xs, Y + 1], (gx, left))),
        )

    def send(parts):
        for sends, gets, copy in parts:
            pl.when(sends)(copy.start)

    def receive(parts):
        for sends, gets, copy in parts:
            pl.when(gets)(copy.wait_recv)

    def sent(parts):
        for sends, gets, copy in parts:
            pl.when(sends)(copy.wait_send)

    loop(X * Y, lambda p: load_u(p).wait())
    pl.semaphore_wait(barrier, nx - 1 + ny - 1)
    border1 = borders(uf, hs1, hr1)
    send(border1)

    def gram(p):
        load_v(p).wait()
        vh, vl = split(vf[p])
        uh, ul = split(uf[p // Y + 1, p % Y + 1])
        high = jnp.concatenate([vh, uh], 0)
        low = jnp.concatenate([vl, ul], 0)
        bh[p, 0:rows, :] = high
        bl[p, 0:rows, :] = low
        r = quick(jnp.concatenate([high, low], 0), high, nt=True)
        acc[0:rows, 0:rows] += r[:rows]
        acc[WIDE : WIDE + rows, 0:rows] += r[rows:]

    loop(X * Y, gram)

    lane = lax.broadcasted_iota(jnp.int32, (BLOCK, Z), 1)

    def image(field, height):
        def step(x):
            total = jnp.zeros((height + BLOCK, 2 * BLOCK), F32)
            for y in range(Y):
                here = field[x + 1, y + 1]
                a0 = adv[0, x, y : y + 1, :]
                a1 = adv[1, x, y : y + 1, :]
                a2 = adv[2, x, y : y + 1, :]
                below = jnp.where(lane == 0, 0.0, pltpu.roll(here, 1, 1))
                above = jnp.where(lane == Z - 1, 0.0, pltpu.roll(here, Z - 1, 1))
                near = (1.0 + a0) * field[x, y + 1] + (1.0 - a0) * field[x + 2, y + 1]
                near = near + (1.0 + a1) * field[x + 1, y] + (1.0 - a1) * field[x + 1, y + 2]
                near = near + (1.0 + a2) * below + (1.0 - a2) * above
                w = (6.0 + rea[x, y : y + 1, :]) * here - near
                p = x * Y + y
                wh, wl = split(w)
                bh[p, height : height + BLOCK, :] = wh
                bl[p, height : height + BLOCK, :] = wl
                both = jnp.concatenate([wh, wl], 0)
                total = total + quick(jnp.concatenate([bh[p, 0:height, :], wh], 0), both, nt=True)
                total = total + quick(jnp.concatenate([bl[p, 0:height, :], wl], 0), both, nt=True)
            hacc[0 : height + BLOCK, 0 : 2 * BLOCK] += total

        loop(X, step)
        turned = hacc[...].T
        return turned[0:BLOCK] + turned[BLOCK : 2 * BLOCK]

    receive(border1)
    dots = image(uf, rows)
    cross = acc[WIDE : 2 * WIDE, :]
    local = acc[0:WIDE, :] + cross + cross.T
    own1[0:main, :] = local[0:main, 0:main]
    own1[main : main + 16, :] = local[main : main + 16, 0:main]
    own1[main + 16 : main + 32, :] = local[main : main + 16, main:WIDE]
    own1[main + 32 : main + 48, :] = dots[:, 0:main]
    own1[main + 48 : main + 64, :] = dots[:, main:WIDE]
    sum_everywhere(nx, ny, own1, first1, part1, second1, done1, whole1, sems[0:6])

    metric[0:main, 0:main] = whole1[0:main, :] * (1.0 / cells)
    metric[main : main + 16, 0:main] = whole1[main : main + 16, :] * (1.0 / cells)
    metric[main : main + 16, main:WIDE] = whole1[main + 16 : main + 32, :] * (1.0 / cells)
    metric[0:main, main:WIDE] = metric[main:WIDE, 0:main].T
    sums = jnp.concatenate([whole1[main + 32 : main + 48, :], whole1[main + 48 : main + 64, :]], 1)
    coeff, upper, combine, left = solve_small(rows, sums, metric[...], cells)
    coeff1[...] = coeff
    upper1[...] = upper

    def assemble(combine, height, put):
        ch, cl = split(combine)
        both = jnp.concatenate([ch, cl], 0)[:, 0:height]

        def step(x):
            for y in range(Y):
                p = x * Y + y
                r = quick(both, bh[p, 0:height, :]) + quick(both, bl[p, 0:height, :])
                put(x, y, p, r[0:BLOCK] + r[BLOCK : 2 * BLOCK])

        loop(X, step)

    def put_one(x, y, p, q):
        qf[x + 1, y + 1] = q
        qh, ql = split(q)
        bh[p, rows : rows + BLOCK, :] = qh
        bl[p, rows : rows + BLOCK, :] = ql

    assemble(combine, rows + BLOCK, put_one)
    border2 = borders(qf, hs2, hr2)
    send(border2)

    def store_one(p):
        x, y = p // Y, p % Y
        return pltpu.make_async_copy(qf.at[x + 1, y + 1], one_hbm.at[:, x, y], osem1.at[p])

    loop(X * Y, lambda p: store_one(p).start())

    extra = jnp.concatenate(
        [jnp.zeros((16, WIDE), F32), left, jnp.zeros((LANES - 32, WIDE), F32)], 0
    )
    metric[main:WIDE, :] += extra
    metric[0:main, main:WIDE] += extra[:, 0:main].T
    r = lax.broadcasted_iota(jnp.int32, (LANES, LANES), 0)
    c = lax.broadcasted_iota(jnp.int32, (LANES, LANES), 1)
    unit = jnp.where((r == c) & (r >= 16) & (r < 32), 1.0, 0.0)
    metric[main:WIDE, main:WIDE] += extra[:, main:WIDE].T + unit

    hacc[...] = jnp.zeros_like(hacc)
    receive(border2)
    dots = image(qf, rows + BLOCK)
    own2[0:16, :] = dots[:, 0:main]
    own2[16:32, :] = dots[:, main:WIDE]
    sum_everywhere(nx, ny, own2, first2, part2, second2, done2, whole2, sems[6:12])
    sums = jnp.concatenate([whole2[0:16, :], whole2[16:32, :]], 1)
    coeff, upper, combine, left = solve_small(rows + BLOCK, sums, metric[...], cells)
    coeff2[...] = coeff
    upper2[...] = upper

    def put_two(x, y, p, q):
        pf[x, y] = q

    assemble(combine, rows + 2 * BLOCK, put_two)

    def store_two(p):
        x, y = p // Y, p % Y
        return pltpu.make_async_copy(pf.at[x, y], two_hbm.at[:, x, y], osem2.at[p])

    loop(X * Y, lambda p: store_two(p).start())
    sent(border1)
    sent(border2)
    loop(X * Y, lambda p: store_one(p).wait())
    loop(X * Y, lambda p: store_two(p).wait())


def body(nx, ny, krylov_basis, advection, reaction):
    rows, X, Y, Z = krylov_basis.shape
    height1 = rows - BLOCK + 64
    height2 = max(32, 8 * nx)
    dma = pltpu.SemaphoreType.DMA
    field = jax.ShapeDtypeStruct((BLOCK, X, Y, Z), F32)
    sum_scratch = []
    for height in (height1, height2):
        sum_scratch += [
            pltpu.VMEM((height, LANES), F32),
            pltpu.VMEM((nx - 1, height // nx, LANES), F32),
            pltpu.VMEM((height // nx, LANES), F32),
            pltpu.VMEM((ny, height // nx, LANES), F32),
            pltpu.VMEM((height // nx, LANES), F32),
            pltpu.VMEM((height, LANES), F32),
        ]
    sum_sems = [dma((n - 1,)) for n in (nx, nx, ny, ny, nx, nx)] * 2
    vmem = pl.BlockSpec(memory_space=pltpu.VMEM)
    hbm = pl.BlockSpec(memory_space=pl.ANY)
    one, two, coeff1, coeff2, upper1, upper2 = pl.pallas_call(
        functools.partial(kernel, nx, ny),
        out_shape=(
            field,
            field,
            jax.ShapeDtypeStruct((BLOCK, WIDE), F32),
            jax.ShapeDtypeStruct((BLOCK, WIDE), F32),
            jax.ShapeDtypeStruct((BLOCK, BLOCK), F32),
            jax.ShapeDtypeStruct((BLOCK, BLOCK), F32),
        ),
        in_specs=[hbm, vmem, vmem],
        out_specs=(hbm, hbm, vmem, vmem, vmem, vmem),
        scratch_shapes=[
            pltpu.VMEM((X * Y, rows - BLOCK, Z), F32),
            pltpu.VMEM((X * Y, rows + 2 * BLOCK, Z), BF16),
            pltpu.VMEM((X * Y, rows + 2 * BLOCK, Z), BF16),
            pltpu.VMEM((X + 2, Y + 2, BLOCK, Z), F32),
            pltpu.VMEM((X + 2, Y + 2, BLOCK, Z), F32),
            pltpu.VMEM((X, Y, BLOCK, Z), F32),
            pltpu.VMEM((2 * WIDE, WIDE), F32),
            pltpu.VMEM((WIDE, LANES), F32),
            pltpu.VMEM((WIDE, WIDE), F32),
        ]
        + sum_scratch
        + [dma((X * Y,))] * 4
        + [dma((4,))] * 4
        + sum_sems,
        compiler_params=pltpu.CompilerParams(
            collective_id=0, has_side_effects=True, vmem_limit_bytes=56 * 1024 * 1024
        ),
    )(krylov_basis, advection, reaction)
    return (one, two, coeff1[:, :rows].T, coeff2[:, : rows + BLOCK].T, upper1, upper2)


def solution(mesh):
    return jax.shard_map(
        functools.partial(body, mesh.shape["gx"], mesh.shape["gy"]),
        mesh=mesh,
        in_specs=(P(None, "gx", "gy", None), P(None, "gx", "gy", None), P("gx", "gy", None)),
        out_specs=(P(None, "gx", "gy", None), P(None, "gx", "gy", None), P(), P(), P(), P()),
        check_vma=False,
    )
```

profile of v0, /device:TPU:0, one launch (start us, length us, event | category | flops | bytes accessed | tf_op | source)
XLA Modules:
  0.0 86.2 jit_solution(6588279800762206339)
XLA Ops:
  0.6 75.8 %shard_map.82 = (f32[16,8,8,256]{3,2,1,0:T(8,128)}, f32[16,8,8,256]{3,2,1,0:T(8,128)}, f32[16,256]{1,0:T(8,128)}, f32[16,256]{1,0:T(8,128)}, f32[16,16]{1,0:T(8,128)}, /*index=5*/f32[16,16]{1,0:T(8,128)}) custom-call(f32[144,8,8,256]{3,2,1,0:T(8,128)} %v_hbm.1, f32[3,8,8,256]{3,2,1,0:T(8,128)} %adv.1, f32[8,8,256]{2,1,0:T(8,128)} %rea.1), custom_call_target="tpu_custom_call" | custom-call | tf_op jit(solution)/shard_map/pallas_call | solution.py:385
  76.4 1.3 %slice_bitcast_fusion.1 = f32[144,16]{0,1:T(8,128)} fusion(f32[16,256]{1,0:T(8,128)} %get-tuple-element.14), kind=kLoop, calls=%fused_computation.1 | loop fusion | bytes 18432 | tf_op jit(solution)/shard_map/transpose | solution.py:416
  77.7 1.3 %slice_bitcast_fusion = f32[160,16]{0,1:T(8,128)} fusion(f32[16,256]{1,0:T(8,128)} %get-tuple-element.15), kind=kLoop, calls=%fused_computation | loop fusion | bytes 20480 | tf_op jit(solution)/shard_map/transpose | solution.py:416
  79.0 2.3 %copy.13 = f32[16,8,8,256]{3,2,1,0:T(8,128)} copy(f32[16,8,8,256]{3,2,1,0:T(8,128)} %get-tuple-element.24) | data formatting | bytes 2097152
  81.3 2.3 %copy.14 = f32[16,8,8,256]{3,2,1,0:T(8,128)} copy(f32[16,8,8,256]{3,2,1,0:T(8,128)} %get-tuple-element.25) | data formatting | bytes 2097152
  83.6 1.3 %copy.15 = f32[16,16]{1,0:T(8,128)} copy(f32[16,16]{1,0:T(8,128)} %get-tuple-element.28) | data formatting | bytes 2048
  84.9 1.3 %copy.16 = f32[16,16]{1,0:T(8,128)} copy(f32[16,16]{1,0:T(8,128)} %get-tuple-element.29) | data formatting | bytes 2048
where the time goes:
time: 86.7 us; the launch traced here: 86.2 us
  Pallas kernels  75.8 us (87%)
  local copies, waits for them, and re-layouts  9.82 us (11%)
    pallas_call x1, Pallas kernels, body(): pl.pallas_call(functools.partial(kernel, nx, ny), out_shape=(field, field...  75.8 us
    unnamed x4, local copies, waits for them, and re-layouts  7.17 us

commit v1 on v0

--- a/solution.py
+++ b/solution.py
@@ -30,6 +30,32 @@
     high = values.astype(BF16)
     low = (values - high.astype(F32)).astype(BF16)
     return high, low
+
+
+def loop(n, f):
+    lax.fori_loop(0, n, lambda i, c: (f(i), c)[1], 0)
+
+
+def over_edges(X, Y, step):
+    loop(2, lambda i: step(i * (X - 1), range(Y)))
+    loop(X - 2, lambda i: step(i + 1, (0, Y - 1)))
+
+
+def over_inside(X, Y, step):
+    loop(X - 2, lambda i: step(i + 1, range(1, Y - 1)))
+
+
+def assemble(bh, bl, X, Y, combine, height, put):
+    ch, cl = split(combine)
+    both = jnp.concatenate([ch, cl], 0)[:, 0:height]
+
+    def step(x, ys):
+        for y in ys:
+            p = x * Y + y
+            r = quick(both, bh[p, 0:height, :]) + quick(both, bl[p, 0:height, :])
+            put(x, y, p, r[0:BLOCK] + r[BLOCK : 2 * BLOCK])
+
+    return step
 
 
 def sum_everywhere(nx, ny, own, first, part, second, done, whole, sems):
@@ -136,12 +162,12 @@
 
 def kernel(
     nx, ny,
-    v_hbm, adv, rea,
-    one_hbm, two_hbm, coeff1, coeff2, upper1, upper2,
-    vf, bh, bl, uf, qf, pf, acc, hacc, metric,
+    v_hbm, adv_hbm, rea_hbm,
+    bh, bl, qf, last, coeff1, coeff2, upper1, upper2,
+    vf, adv, rea, uf, acc, hacc, metric,
     own1, first1, part1, second1, done1, whole1,
     own2, first2, part2, second2, done2, whole2,
-    vsem, usem, osem1, osem2, hs1, hr1, hs2, hr2,
+    vsem, usem, asem, hs1, hr1, hs2, hr2,
     *sems,
 ):
     rows, X, Y, Z = v_hbm.shape
@@ -156,14 +182,19 @@
         )
 
     def load_v(p):
-        x, y = p // Y, p % Y
-        return pltpu.make_async_copy(v_hbm.at[pl.ds(0, main), x, y], vf.at[p], vsem.at[p])
-
-    def loop(n, f):
-        lax.fori_loop(0, n, lambda i, c: (f(i), c)[1], 0)
+        x, half = p // 2, p % 2
+        lanes = pl.ds(pl.multiple_of(half * LANES, LANES), LANES)
+        return pltpu.make_async_copy(v_hbm.at[pl.ds(0, main), x, :, lanes], vf.at[p], vsem.at[p])
 
     loop(X * Y, lambda p: load_u(p).start())
-    loop(X * Y, lambda p: load_v(p).start())
+    loop(2 * X, lambda p: load_v(p).start())
+
+    fetches = (
+        pltpu.make_async_copy(adv_hbm, adv, asem.at[0]),
+        pltpu.make_async_copy(rea_hbm, rea, asem.at[1]),
+    )
+    for fetch in fetches:
+        fetch.start()
 
     barrier = pltpu.get_barrier_semaphore()
     for d in range(1, nx):
@@ -231,30 +262,35 @@
             pl.when(sends)(copy.wait_send)
 
     loop(X * Y, lambda p: load_u(p).wait())
+
+    def gram(x):
+        load_v(2 * x).wait()
+        load_v(2 * x + 1).wait()
+        slabs = [vf.at[2 * x + i].reshape(main * Y, LANES) for i in range(2)]
+        for y in range(Y):
+            p = x * Y + y
+            vh, vl = split(jnp.concatenate([slab[pl.ds(y, main, stride=Y), :] for slab in slabs], 1))
+            uh, ul = split(uf[x + 1, y + 1])
+            high = jnp.concatenate([vh, uh], 0)
+            low = jnp.concatenate([vl, ul], 0)
+            bh[p, 0:rows, :] = high
+            bl[p, 0:rows, :] = low
+            r = quick(jnp.concatenate([high, low], 0), high, nt=True)
+            acc[0:rows, 0:rows] += r[:rows]
+            acc[WIDE : WIDE + rows, 0:rows] += r[rows:]
+
+    gram(0)
     pl.semaphore_wait(barrier, nx - 1 + ny - 1)
     border1 = borders(uf, hs1, hr1)
     send(border1)
-
-    def gram(p):
-        load_v(p).wait()
-        vh, vl = split(vf[p])
-        uh, ul = split(uf[p // Y + 1, p % Y + 1])
-        high = jnp.concatenate([vh, uh], 0)
-        low = jnp.concatenate([vl, ul], 0)
-        bh[p, 0:rows, :] = high
-        bl[p, 0:rows, :] = low
-        r = quick(jnp.concatenate([high, low], 0), high, nt=True)
-        acc[0:rows, 0:rows] += r[:rows]
-        acc[WIDE : WIDE + rows, 0:rows] += r[rows:]
-
-    loop(X * Y, gram)
+    loop(X - 1, lambda i: gram(i + 1))
 
     lane = lax.broadcasted_iota(jnp.int32, (BLOCK, Z), 1)
 
-    def image(field, height):
-        def step(x):
+    def image(field, height, border):
+        def step(x, ys):
             total = jnp.zeros((height + BLOCK, 2 * BLOCK), F32)
-            for y in range(Y):
+            for y in ys:
                 here = field[x + 1, y + 1]
                 a0 = adv[0, x, y : y + 1, :]
                 a1 = adv[1, x, y : y + 1, :]
@@ -274,12 +310,15 @@
                 total = total + quick(jnp.concatenate([bl[p, 0:height, :], wl], 0), both, nt=True)
             hacc[0 : height + BLOCK, 0 : 2 * BLOCK] += total
 
-        loop(X, step)
+        over_inside(X, Y, step)
+        receive(border)
+        over_edges(X, Y, step)
         turned = hacc[...].T
         return turned[0:BLOCK] + turned[BLOCK : 2 * BLOCK]
 
-    receive(border1)
-    dots = image(uf, rows)
+    for fetch in fetches:
+        fetch.wait()
+    dots = image(uf, rows, border1)
     cross = acc[WIDE : 2 * WIDE, :]
     local = acc[0:WIDE, :] + cross + cross.T
     own1[0:main, :] = local[0:main, 0:main]
@@ -298,33 +337,17 @@
     coeff1[...] = coeff
     upper1[...] = upper
 
-    def assemble(combine, height, put):
-        ch, cl = split(combine)
-        both = jnp.concatenate([ch, cl], 0)[:, 0:height]
-
-        def step(x):
-            for y in range(Y):
-                p = x * Y + y
-                r = quick(both, bh[p, 0:height, :]) + quick(both, bl[p, 0:height, :])
-                put(x, y, p, r[0:BLOCK] + r[BLOCK : 2 * BLOCK])
-
-        loop(X, step)
-
     def put_one(x, y, p, q):
         qf[x + 1, y + 1] = q
         qh, ql = split(q)
         bh[p, rows : rows + BLOCK, :] = qh
         bl[p, rows : rows + BLOCK, :] = ql
 
-    assemble(combine, rows + BLOCK, put_one)
+    step_one = assemble(bh, bl, X, Y, combine, rows + BLOCK, put_one)
+    over_edges(X, Y, step_one)
     border2 = borders(qf, hs2, hr2)
     send(border2)
-
-    def store_one(p):
-        x, y = p // Y, p % Y
-        return pltpu.make_async_copy(qf.at[x + 1, y + 1], one_hbm.at[:, x, y], osem1.at[p])
-
-    loop(X * Y, lambda p: store_one(p).start())
+    over_inside(X, Y, step_one)
 
     extra = jnp.concatenate(
         [jnp.zeros((16, WIDE), F32), left, jnp.zeros((LANES - 32, WIDE), F32)], 0
@@ -337,8 +360,7 @@
     metric[main:WIDE, main:WIDE] += extra[:, main:WIDE].T + unit
 
     hacc[...] = jnp.zeros_like(hacc)
-    receive(border2)
-    dots = image(qf, rows + BLOCK)
+    dots = image(qf, rows + BLOCK, border2)
     own2[0:16, :] = dots[:, 0:main]
     own2[16:32, :] = dots[:, main:WIDE]
     sum_everywhere(nx, ny, own2, first2, part2, second2, done2, whole2, sems[6:12])
@@ -347,18 +369,43 @@
     coeff2[...] = coeff
     upper2[...] = upper
 
-    def put_two(x, y, p, q):
-        pf[x, y] = q
-
-    assemble(combine, rows + 2 * BLOCK, put_two)
+    last[...] = combine
+    sent(border1)
+    sent(border2)
+
+
+def finish(
+    bh, bl, qf, last, coeff1, coeff2, upper1, upper2,
+    one_hbm, two_hbm, out1, out2, factor1, factor2,
+    pf, sem1, sem2,
+):
+    _, X, Y, _ = one_hbm.shape
+
+    def store_one(p):
+        x, y = p // Y, p % Y
+        return pltpu.make_async_copy(qf.at[x + 1, y + 1], one_hbm.at[:, x, y], sem1.at[p])
 
     def store_two(p):
         x, y = p // Y, p % Y
-        return pltpu.make_async_copy(pf.at[x, y], two_hbm.at[:, x, y], osem2.at[p])
-
-    loop(X * Y, lambda p: store_two(p).start())
-    sent(border1)
-    sent(border2)
+        return pltpu.make_async_copy(pf.at[p], two_hbm.at[:, x, y], sem2.at[p])
+
+    loop(X * Y, lambda p: store_one(p).start())
+
+    def put_two(x, y, p, q):
+        pf[p] = q
+
+    step_two = assemble(bh, bl, X, Y, last[...], bh.shape[1], put_two)
+
+    def finish_slab(x):
+        step_two(x, range(Y))
+        loop(Y, lambda y: store_two(x * Y + y).start())
+
+    loop(X, finish_slab)
+    rows1, rows2 = out1.shape[1], out2.shape[1]
+    out1[...] = coeff1[:, 0:rows1]
+    out2[...] = coeff2[:, 0:rows2]
+    factor1[...] = upper1[...]
+    factor2[...] = upper2[...]
     loop(X * Y, lambda p: store_one(p).wait())
     loop(X * Y, lambda p: store_two(p).wait())
 
@@ -382,38 +429,56 @@
     sum_sems = [dma((n - 1,)) for n in (nx, nx, ny, ny, nx, nx)] * 2
     vmem = pl.BlockSpec(memory_space=pltpu.VMEM)
     hbm = pl.BlockSpec(memory_space=pl.ANY)
-    one, two, coeff1, coeff2, upper1, upper2 = pl.pallas_call(
+    parts = ((X * Y, rows + 2 * BLOCK, Z), BF16)
+    limit = 28 * 1024 * 1024
+    results = pl.pallas_call(
         functools.partial(kernel, nx, ny),
         out_shape=(
-            field,
-            field,
-            jax.ShapeDtypeStruct((BLOCK, WIDE), F32),
-            jax.ShapeDtypeStruct((BLOCK, WIDE), F32),
-            jax.ShapeDtypeStruct((BLOCK, BLOCK), F32),
-            jax.ShapeDtypeStruct((BLOCK, BLOCK), F32),
+            pltpu.VMEM(*parts),
+            pltpu.VMEM(*parts),
+            pltpu.VMEM((X + 2, Y + 2, BLOCK, Z), F32),
+            pltpu.VMEM((BLOCK, WIDE), F32),
+            pltpu.VMEM((BLOCK, WIDE), F32),
+            pltpu.VMEM((BLOCK, WIDE), F32),
+            pltpu.VMEM((BLOCK, BLOCK), F32),
+            pltpu.VMEM((BLOCK, BLOCK), F32),
         ),
-        in_specs=[hbm, vmem, vmem],
-        out_specs=(hbm, hbm, vmem, vmem, vmem, vmem),
+        in_specs=[pl.BlockSpec(memory_space=pltpu.HBM)] * 3,
+        out_specs=(vmem,) * 8,
         scratch_shapes=[
-            pltpu.VMEM((X * Y, rows - BLOCK, Z), F32),
-            pltpu.VMEM((X * Y, rows + 2 * BLOCK, Z), BF16),
-            pltpu.VMEM((X * Y, rows + 2 * BLOCK, Z), BF16),
+            pltpu.VMEM((2 * X, rows - BLOCK, Y, LANES), F32),
+            pltpu.VMEM((3, X, Y, Z), F32),
+            pltpu.VMEM((X, Y, Z), F32),
             pltpu.VMEM((X + 2, Y + 2, BLOCK, Z), F32),
-            pltpu.VMEM((X + 2, Y + 2, BLOCK, Z), F32),
-            pltpu.VMEM((X, Y, BLOCK, Z), F32),
             pltpu.VMEM((2 * WIDE, WIDE), F32),
             pltpu.VMEM((WIDE, LANES), F32),
             pltpu.VMEM((WIDE, WIDE), F32),
         ]
         + sum_scratch
-        + [dma((X * Y,))] * 4
+        + [dma((X * Y,))] * 2
+        + [dma((2,))]
         + [dma((4,))] * 4
         + sum_sems,
         compiler_params=pltpu.CompilerParams(
-            collective_id=0, has_side_effects=True, vmem_limit_bytes=56 * 1024 * 1024
+            collective_id=0, has_side_effects=True, vmem_limit_bytes=limit
         ),
-    )(krylov_basis, advection, reaction)
-    return (one, two, coeff1[:, :rows].T, coeff2[:, : rows + BLOCK].T, upper1, upper2)
+    )(*(pltpu.with_memory_space_constraint(a, pltpu.HBM) for a in (krylov_basis, advection, reaction)))
+    one, two, out1, out2, factor1, factor2 = pl.pallas_call(
+        finish,
+        out_shape=(
+            field,
+            field,
+            jax.ShapeDtypeStruct((BLOCK, rows), F32),
+            jax.ShapeDtypeStruct((BLOCK, rows + BLOCK), F32),
+            jax.ShapeDtypeStruct((BLOCK, BLOCK), F32),
+            jax.ShapeDtypeStruct((BLOCK, BLOCK), F32),
+        ),
+        in_specs=[vmem] * 8,
+        out_specs=(hbm, hbm, vmem, vmem, vmem, vmem),
+        scratch_shapes=[pltpu.VMEM((X * Y, BLOCK, Z), F32), dma((X * Y,)), dma((X * Y,))],
+        compiler_params=pltpu.CompilerParams(vmem_limit_bytes=limit),
+    )(*results)
+    return one, two, out1.T, out2.T, factor1, factor2
 
 
 def solution(mesh):

time: 86.7 us -> 66.2 us (0.76)
  Pallas kernels: 75.8 us -> 65.4 us
  local copies, waits for them, and re-layouts: 9.82 us -> 0 us
    pallas_call x1 -> x2, Pallas kernels: 75.8 us -> 65.4 us  [the longest x1 58.5 us: body(): pl.pallas_call(functools.partial(kernel, nx, ny), out_shape=(pltpu.VMEM(*...]
    unnamed x4 -> x0, local copies, waits for them, and re-layouts: 7.17 us -> none
    transpose x2 -> x0, local copies, waits for them, and re-layouts: 2.65 us -> none  [the longest x1 1.32 us: body(): coeff1[:, :rows]]
where the time goes in v1:
time: 66.2 us; the launch traced here: 66.1 us
  Pallas kernels  65.4 us (99%)
    pallas_call x1, Pallas kernels, body(): pl.pallas_call(functools.partial(kernel, nx, ny), out_shape=(pltpu.VMEM(*...  58.5 us
    pallas_call x1, Pallas kernels, body(): pl.pallas_call(finish, out_shape=(field, field, jax.ShapeDtypeStruct((BLO...  6.92 us

profile of v1, /device:TPU:0, one launch (start us, length us, event | category | flops | bytes accessed | tf_op | source)
XLA Modules:
  0.0 66.1 jit_solution(16170775772303190091)
XLA Ops:
  0.6 58.5 %shard_map.82 = (bf16[64,176,256]{2,1,0:T(8,128)(2,1)S(1)}, bf16[64,176,256]{2,1,0:T(8,128)(2,1)S(1)}, f32[10,10,16,256]{3,2,1,0:T(8,128)S(1)}, f32[16,256]{1,0:...) custom-call(f32[144,8,8,256]{3,2,1,0:T(8,128)} %v_hbm.1, ...), custom_call_target="tpu_custom_call" | custom-call | tf_op jit(solution)/shard_map/pallas_call | solution.py:434
  59.2 6.9 %shard_map.83 = (f32[16,8,8,256]{3,2,1,0:T(8,128)}, f32[16,8,8,256]{3,2,1,0:T(8,128)}, f32[16,144]{1,0:T(8,128)}, f32[16,160]{1,0:T(8,128)}, f32[16,16]{1,0:T(8,128)}, /*index=5*/f32[16,16]{1,0:T(8,128)}) custom-call(bf16[64,176,256]{2,1,0:T(8,128)(2,1)S(1)} %get-tuple-element.20.bh, bf16[64,176,256]{2,1,0:T(8,128)(2,1)S(1)} %get-tuple-element.21.bl, ...), custom_call_target="tpu_custom_call" | custom-call | tf_op jit(solution)/shard_map/pallas_call | solution.py:466

commit v2 on v1

--- a/solution.py
+++ b/solution.py
@@ -78,6 +78,7 @@
         )
     for copy in copies:
         copy.start()
+    yield
     for copy in copies:
         copy.wait_recv()
     total = own[mine, :]
@@ -100,6 +101,7 @@
         )
     for copy in across:
         copy.start()
+    yield
     for copy in across:
         copy.wait_recv()
     total = second[0]
@@ -122,10 +124,12 @@
         )
     for copy in back:
         copy.start()
+    yield
     for copy in back:
         copy.wait_recv()
     for copy in copies + across + back:
         copy.wait_send()
+    yield
 
 
 def factor(gram):
@@ -167,6 +171,7 @@
     vf, adv, rea, uf, acc, hacc, metric,
     own1, first1, part1, second1, done1, whole1,
     own2, first2, part2, second2, done2, whole2,
+    own3, first3, part3, second3, done3, whole3,
     vsem, usem, asem, hs1, hr1, hs2, hr2,
     *sems,
 ):
@@ -211,6 +216,7 @@
     metric[...] = jnp.zeros_like(metric)
     own1[...] = jnp.zeros_like(own1)
     own2[...] = jnp.zeros_like(own2)
+    own3[...] = jnp.zeros_like(own3)
     edge_x = jnp.zeros((1, Y, BLOCK, Z), F32)
     edge_y = jnp.zeros((X, 1, BLOCK, Z), F32)
     for field in (uf, qf):
@@ -287,7 +293,7 @@
 
     lane = lax.broadcasted_iota(jnp.int32, (BLOCK, Z), 1)
 
-    def image(field, height, border):
+    def image(field, height, border, between=None):
         def step(x, ys):
             total = jnp.zeros((height + BLOCK, 2 * BLOCK), F32)
             for y in ys:
@@ -312,27 +318,37 @@
 
         over_inside(X, Y, step)
         receive(border)
+        if between is not None:
+            next(between)
         over_edges(X, Y, step)
         turned = hacc[...].T
         return turned[0:BLOCK] + turned[BLOCK : 2 * BLOCK]
 
     for fetch in fetches:
         fetch.wait()
-    dots = image(uf, rows, border1)
     cross = acc[WIDE : 2 * WIDE, :]
     local = acc[0:WIDE, :] + cross + cross.T
     own1[0:main, :] = local[0:main, 0:main]
     own1[main : main + 16, :] = local[main : main + 16, 0:main]
     own1[main + 16 : main + 32, :] = local[main : main + 16, main:WIDE]
-    own1[main + 32 : main + 48, :] = dots[:, 0:main]
-    own1[main + 48 : main + 64, :] = dots[:, main:WIDE]
-    sum_everywhere(nx, ny, own1, first1, part1, second1, done1, whole1, sems[0:6])
+    bases_sum = sum_everywhere(nx, ny, own1, first1, part1, second1, done1, whole1, sems[0:6])
+    next(bases_sum)
+    dots = image(uf, rows, border1, bases_sum)
+    own2[0:16, :] = dots[:, 0:main]
+    own2[16:32, :] = dots[:, main:WIDE]
+    image_sum = sum_everywhere(nx, ny, own2, first2, part2, second2, done2, whole2, sems[6:12])
+    next(image_sum)
+    next(bases_sum)
+    next(image_sum)
+    next(bases_sum)
+    next(image_sum)
+    next(image_sum)
 
     metric[0:main, 0:main] = whole1[0:main, :] * (1.0 / cells)
     metric[main : main + 16, 0:main] = whole1[main : main + 16, :] * (1.0 / cells)
     metric[main : main + 16, main:WIDE] = whole1[main + 16 : main + 32, :] * (1.0 / cells)
     metric[0:main, main:WIDE] = metric[main:WIDE, 0:main].T
-    sums = jnp.concatenate([whole1[main + 32 : main + 48, :], whole1[main + 48 : main + 64, :]], 1)
+    sums = jnp.concatenate([whole2[0:16, :], whole2[16:32, :]], 1)
     coeff, upper, combine, left = solve_small(rows, sums, metric[...], cells)
     coeff1[...] = coeff
     upper1[...] = upper
@@ -361,10 +377,11 @@
 
     hacc[...] = jnp.zeros_like(hacc)
     dots = image(qf, rows + BLOCK, border2)
-    own2[0:16, :] = dots[:, 0:main]
-    own2[16:32, :] = dots[:, main:WIDE]
-    sum_everywhere(nx, ny, own2, first2, part2, second2, done2, whole2, sems[6:12])
-    sums = jnp.concatenate([whole2[0:16, :], whole2[16:32, :]], 1)
+    own3[0:16, :] = dots[:, 0:main]
+    own3[16:32, :] = dots[:, main:WIDE]
+    for _ in sum_everywhere(nx, ny, own3, first3, part3, second3, done3, whole3, sems[12:18]):
+        pass
+    sums = jnp.concatenate([whole3[0:16, :], whole3[16:32, :]], 1)
     coeff, upper, combine, left = solve_small(rows + BLOCK, sums, metric[...], cells)
     coeff2[...] = coeff
     upper2[...] = upper
@@ -412,12 +429,12 @@
 
 def body(nx, ny, krylov_basis, advection, reaction):
     rows, X, Y, Z = krylov_basis.shape
-    height1 = rows - BLOCK + 64
+    height1 = -(-(rows + BLOCK) // (8 * nx)) * (8 * nx)
     height2 = max(32, 8 * nx)
     dma = pltpu.SemaphoreType.DMA
     field = jax.ShapeDtypeStruct((BLOCK, X, Y, Z), F32)
     sum_scratch = []
-    for height in (height1, height2):
+    for height in (height1, height2, height2):
         sum_scratch += [
             pltpu.VMEM((height, LANES), F32),
             pltpu.VMEM((nx - 1, height // nx, LANES), F32),
@@ -426,7 +443,7 @@
             pltpu.VMEM((height // nx, LANES), F32),
             pltpu.VMEM((height, LANES), F32),
         ]
-    sum_sems = [dma((n - 1,)) for n in (nx, nx, ny, ny, nx, nx)] * 2
+    sum_sems = [dma((n - 1,)) for n in (nx, nx, ny, ny, nx, nx)] * 3
     vmem = pl.BlockSpec(memory_space=pltpu.VMEM)
     hbm = pl.BlockSpec(memory_space=pl.ANY)
     parts = ((X * Y, rows + 2 * BLOCK, Z), BF16)

time: 66.2 us -> 64.5 us (0.974)
  Pallas kernels: 65.4 us -> 63.7 us
    pallas_call x1, Pallas kernels: 58.5 us -> 56.8 us  [body(): pl.pallas_call(functools.partial(kernel, nx, ny), out_shape=(pltpu.VMEM(*...]
where the time goes in v2:
time: 64.5 us; the launch traced here: 64.3 us
  Pallas kernels  63.7 us (99%)
    pallas_call x1, Pallas kernels, body(): pl.pallas_call(functools.partial(kernel, nx, ny), out_shape=(pltpu.VMEM(*...  56.8 us
    pallas_call x1, Pallas kernels, body(): pl.pallas_call(finish, out_shape=(field, field, jax.ShapeDtypeStruct((BLO...  6.91 us

profile of v2, /device:TPU:0, one launch (start us, length us, event | category | flops | bytes accessed | tf_op | source)
XLA Modules:
  0.0 64.3 jit_solution(635667285206137196)
XLA Ops:
  0.6 56.8 %shard_map.82 = (bf16[64,176,256]{2,1,0:T(8,128)(2,1)S(1)}, bf16[64,176,256]{2,1,0:T(8,128)(2,1)S(1)}, f32[10,10,16,256]{3,2,1,0:T(8,128)S(1)}, f32[16,256]{1,0:...) custom-call(f32[144,8,8,256]{3,2,1,0:T(8,128)} %v_hbm.1, ...), custom_call_target="tpu_custom_call" | custom-call | tf_op jit(solution)/shard_map/pallas_call | solution.py:451
  57.4 6.9 %shard_map.83 = (f32[16,8,8,256]{3,2,1,0:T(8,128)}, f32[16,8,8,256]{3,2,1,0:T(8,128)}, f32[16,144]{1,0:T(8,128)}, f32[16,160]{1,0:T(8,128)}, f32[16,16]{1,0:T(8,128)}, /*index=5*/f32[16,16]{1,0:T(8,128)}) custom-call(bf16[64,176,256]{2,1,0:T(8,128)(2,1)S(1)} %get-tuple-element.20.bh, bf16[64,176,256]{2,1,0:T(8,128)(2,1)S(1)} %get-tuple-element.21.bl, ...), custom_call_target="tpu_custom_call" | custom-call | tf_op jit(solution)/shard_map/pallas_call | solution.py:483
